TPU v7x, 16 devices: a whole 2x2x2 slice. The times are simulated.
16 devices in a mesh: rep: 1, dp: 16 (over x, y, z, core).
Axes of the slice: x: 2, y: 2, z: 2, core: 2. Of those that a mesh axis runs over, the one named last changes fastest.
Arguments:
- x: bfloat16 [16, 2048, 1536], P(('rep', 'dp'))
- dy: bfloat16 [16, 2048, 1536], P(('rep', 'dp'))
- w_gate: bfloat16 [2, 1536, 4096], replicated
- w_up: bfloat16 [2, 1536, 4096], replicated
- w_down: bfloat16 [2, 4096, 1536], replicated
- m_w_gate: float32 [2, 1536, 4096], P(None, 'dp')
- m_w_up: float32 [2, 1536, 4096], P(None, 'dp')
- m_w_down: float32 [2, 4096, 1536], P(None, 'dp')
- v_w_gate: float32 [2, 1536, 4096], P(None, 'dp')
- v_w_up: float32 [2, 1536, 4096], P(None, 'dp')
- v_w_down: float32 [2, 4096, 1536], P(None, 'dp')
Outputs:
- output 1: bfloat16 [2, 1536, 4096], P('rep')
- output 2: bfloat16 [2, 1536, 4096], P('rep')
- output 3: bfloat16 [2, 4096, 1536], P('rep')
- output 4: float32 [2, 1536, 4096], P('rep', 'dp')
- output 5: float32 [2, 1536, 4096], P('rep', 'dp')
- output 6: float32 [2, 4096, 1536], P('rep', 'dp')
- output 7: float32 [2, 1536, 4096], P('rep', 'dp')
- output 8: float32 [2, 1536, 4096], P('rep', 'dp')
- output 9: float32 [2, 4096, 1536], P('rep', 'dp')
All inputs are finite; a program needn't handle non-finite values.
Results may differ from a plain program's by a relative error of at most 0.02.
Values are sent between devices in bfloat16 or wider.
A program may use at most 2 GiB of HBM per device.

v0:
```python
import jax
import jax.numpy as jnp
from jax import lax

NAMES = ("w_gate", "w_up", "w_down")


def matmul(a, w):
    return jnp.dot(a, w, preferred_element_type=jnp.float32).astype(jnp.bfloat16)


def normed(h):
    wide = h.astype(jnp.float32)
    scale = lax.rsqrt(jnp.mean(wide**2, -1, keepdims=True) + 1e-6)
    return (wide * scale).astype(jnp.bfloat16)


def layer(h, w):
    a = normed(h)
    gate = jnp.dot(a, w["w_gate"], preferred_element_type=jnp.float32)
    up = jnp.dot(a, w["w_up"], preferred_element_type=jnp.float32)
    return h + matmul((jax.nn.silu(gate) * up).astype(jnp.bfloat16), w["w_down"])


def adamw(w, m, v, g):
    m = 0.9 * m + 0.1 * g
    v = 0.95 * v + 0.05 * g * g
    step = m * lax.rsqrt(v + 1e-8) + 0.1 * w
    return (w - 0.02 * step).astype(jnp.bfloat16), m, v


def stack(weights, h):
    for number in range(weights["w_gate"].shape[0]):
        h = layer(h, {name: w[number] for name, w in weights.items()})
    return h


def solution(mesh):
    groups = mesh.shape["rep"]

    def step(x, dy, *arrays):
        weights, m, v = (arrays[i : i + 3] for i in (0, 3, 6))
        x, dy = (t.reshape(groups, -1, *t.shape[1:]) for t in (x, dy))

        def of_a_group(x, dy):
            _, back = jax.vjp(lambda w: stack(w, x), dict(zip(NAMES, weights, strict=True)))
            by_weights = back(dy)[0]
            gradients = [by_weights[name].astype(jnp.float32) for name in NAMES]
            new = [adamw(w.astype(jnp.float32), m, v, g) for w, m, v, g in zip(weights, m, v, gradients, strict=True)]
            return tuple(one[which] for which in range(3) for one in new)

        return tuple(t.reshape(-1, *t.shape[2:]) for t in jax.vmap(of_a_group)(x, dy))

    return step
```

profile of v0, /device:TPU:0, one launch (start us, length us, event | category | flops | bytes accessed | tf_op | source)
XLA Modules:
  0.0 2908.8 jit_solution(18032465667948374652)
XLA Ops:
  25.3 33.0 %fusion.173 = f32[2048,4096]{1,0:T(8,128)} fusion(bf16[2,1536,4096]{2,1,0:T(8,128)(2,1)} %param.12, bf16[1,2048,1536]{1,2,0:T(8,128)(2,1)S(1)} %fusion.157), kind=kOutput, calls=%fused_computation.224 | convolution fusion | flops 25769803776 | bytes 52428800 | tf_op jit(solution)/vmap(jvp())/dot_general | solution.py:20
  58.3 43.8 %fusion.150 = (bf16[1,2048,4096]{2,1,0:T(8,128)(2,1)}, f32[2048,4096]{1,0:T(8,128)}) fusion(f32[2048,4096]{1,0:T(8,128)} %fusion.173, bf16[2,1536,4096]{2,1,0:T(8,128)(2,1)} %param.17, bf16[1,2048,1536]{1,2,0:T(8,128)(2,1)} %copy-done), kind=kOutput, calls=%fused_computation.189 | convolution fusion | flops 25820135424 | bytes 102760448 | tf_op jit(solution)/vmap(jvp())/dot_general | solution.py:21
  102.1 47.6 %fusion.160 = (f32[2048]{0:T(1024)S(1)}, bf16[1,2048,1536]{1,2,0:T(8,128)(2,1)}) fusion(bf16[1,2048,1536]{1,2,0:T(8,128)(2,1)} %copy.1, bf16[2,4096,1536]{2,1,0:T(8,128)(2,1)} %param.15, bf16[1,2048,4096]{2,1,0:T(8,128)(2,1)} %get-tuple-element.263), kind=kOutput, calls=%fused_computation.211 | convolution fusion | flops 25785530368 | bytes 41951232 | tf_op jit(solution)/vmap(jvp())/dot_general | solution.py:9
  155.0 35.1 %fusion.166 = f32[2048,4096]{1,0:T(8,128)} fusion(bf16[2,1536,4096]{2,1,0:T(8,128)(2,1)} %param.17, bf16[1,2048,1536]{1,2,0:T(8,128)(2,1)S(1)} %fusion.161), kind=kOutput, calls=%fused_computation.217 | convolution fusion | flops 25769803776 | bytes 52428800 | tf_op jit(solution)/vmap(jvp())/dot_general | solution.py:21
  190.1 31.1 %convolution_convert_fusion.1 = bf16[2048,4096]{1,0:T(8,128)(2,1)} fusion(bf16[2,4096,1536]{2,1,0:T(8,128)(2,1)} %param.15, bf16[1,2048,1536]{2,1,0:T(8,128)(2,1)S(1)} %bitcast.640), kind=kOutput, calls=%fused_computation.206 | convolution fusion | flops 25778192384 | bytes 35651584 | tf_op jit(solution)/vmap(transpose(jvp()))/dot_general | solution.py:9
  221.2 56.3 %fusion.139 = (bf16[1,2048,4096]{2,1,0:T(8,128)(2,1)}, bf16[1,2048,4096]{2,1,0:T(8,128)(2,1)}, f32[2048,4096]{1,0:T(8,128)}) fusion(f32[2048,4096]{1,0:T(8,128)} %fusion.166, bf16[2048,4096]{1,0:T(8,128)(2,1)} %convolution_convert_fusion.1, bf16[2,1536,4096]{2,1,0:T(8,128)(2,1)} %param.12, bf16[1,2048,1536]{1,2,0:T(8,128)(2,1)S(1)} %fusion.161), kind=kOutput, calls=%fused_computation.173 | convolution fusion | flops 25895632896 | bytes 136314880 | tf_op jit(solution)/vmap(jvp())/dot_general | solution.py:20
  277.6 27.5 fusion.149
  305.1 23.0 copy.3
  328.1 324.1 %while.16 = (bf16[1,2048,4096]{1,2,0:T(8,128)(2,1)}, bf16[1,2048,1536]{2,1,0:T(8,128)(2,1)}, f32[256,1536]{1,0:T(8,128)S(1)}, f32[256,1536]{1,0:T(8,128)}, u32[]...) while((bf16[1,2048,4096]{1,2,0:T(8,128)(2,1)}, ...), condition=%wide.windowed_dot_general_cond_rs.4.clone, body=%wide.windowed_dot_general_body_rs.4.clone.sunk | while | flops 6453198848 | bytes 102761032 | solution.py:9
  356.4 32.4 %collective-permute-start.18 = (f32[256,1536]{1,0:T(8,128)}, f32[256,1536]{1,0:T(8,128)S(1)}, u32[]{:S(2)}, u32[]{:S(2)}) collective-permute-start(f32[256,1536]{1,0:T(8,128)} %get-tuple-element.491), channel_id=31, source_target_pairs={{0,1},{1,2},{2,3},{3,4},{4,5},{5,6},{6,7},{7,8},{8,9},{9,10},{10,1... | collective-permute-start | bytes 4718600 | tf_op jit(solution)/vmap(transpose(jvp()))/dot_general | solution.py:9
  492.3 17.6 collective-permute-start.16
  573.5 17.8 collective-permute-start.16
  652.2 17.5 collective-permute-start.28
  678.4 22.6 copy.5
  701.0 34.2 %fusion.190 = bf16[2048,1536]{0,1:T(8,128)(2,1)} fusion(bf16[2,1536,4096]{2,1,0:T(8,128)(2,1)} %param.17, bf16[1,2048,4096]{2,1,0:T(8,128)(2,1)} %get-tuple-element.612), kind=kOutput, calls=%fused_computation.237 | convolution fusion | flops 25769803776 | bytes 35651584 | tf_op jit(solution)/vmap(transpose(jvp()))/dot_general | solution.py:21
  735.2 36.7 %fusion.162 = (f32[2048]{0:T(1024)S(1)}, bf16[2048,1536]{0,1:T(8,128)(2,1)}) fusion(bf16[1,2048,1536]{1,2,0:T(8,128)(2,1)} %get-tuple-element.266, bf16[2048,1536]{0,1:T(8,128)(2,1)} %fusion.190, bf16[2,1536,4096]{2,1,0:T(8,128)(2,1)} %param.12, bf16[1,2048,4096]{2,1,0:T(8,128)(2,1)} %get-tuple-element.540), kind=kOutput, calls=%fused_computation.213 | convolution fusion | flops 25785530368 | bytes 48242688 | tf_op jit(solution)/vmap(transpose(jvp()))/dot_general | solution.py:20
  792.4 325.9 %while.17 = (bf16[1,2048,1536]{2,1,0:T(8,128)(2,1)}, bf16[1,2048,4096]{1,2,0:T(8,128)(2,1)}, f32[1536,256]{0,1:T(8,128)S(1)}, f32[1536,256]{0,1:T(8,128)}, u32[]...) while((bf16[1,2048,1536]{2,1,0:T(8,128)(2,1)}, ...), condition=%wide.windowed_dot_general_cond_rs.5.clone, body=%wide.windowed_dot_general_body_rs.5.clone.sunk | while | flops 6453198848 | bytes 102761032 | solution.py:9
  820.0 32.4 %collective-permute-start.22 = (f32[1536,256]{0,1:T(8,128)}, f32[1536,256]{0,1:T(8,128)}, u32[]{:S(2)}, u32[]{:S(2)}) collective-permute-start(f32[1536,256]{0,1:T(8,128)} %get-tuple-element.500), channel_id=37, source_target_pairs={{0,1},{1,2},{2,3},{3,4},{4,5},{5,6},{6,7},{7,8},{8,9},{9,10},{10,1... | collective-permute-start | bytes 4718600 | tf_op jit(solution)/vmap(transpose(jvp()))/dot_general | solution.py:9
  956.5 17.5 collective-permute-start.20
  1038.4 17.9 collective-permute-start.20
  1118.3 17.5 collective-permute-start.29
  1147.0 389.8 %while.14 = (bf16[1,2048,4096]{2,1,0:T(8,128)(2,1)}, bf16[1,2048,1536]{1,2,0:T(8,128)(2,1)}, f32[4096,96]{0,1:T(8,128)S(1)}, f32[4096,96]{0,1:T(8,128)}, u32[]{:...) while((bf16[1,2048,4096]{2,1,0:T(8,128)(2,1)}, ...), condition=%wide.windowed_dot_general_cond_rs.2.clone, body=%wide.windowed_dot_general_body_rs.2.clone.sunk | while | flops 6447955968 | bytes 102761032 | solution.py:21
  1173.1 21.4 collective-permute-done.9
  1197.5 27.6 collective-permute-start.10
  1251.5 37.4 %collective-permute-start.8 = (f32[4096,96]{0,1:T(8,128)}, f32[4096,96]{0,1:T(8,128)S(1)}, u32[]{:S(2)}, u32[]{:S(2)}) collective-permute-start(f32[4096,96]{0,1:T(8,128)} %broadcast_select_fusion.28), channel_id=16, source_target_pairs={{0,1},{1,2},{2,3},{3,4},{4,5},{5,6},{6,7},{7,8},{8,9},{9,10},{10,1... | collective-permute-start | bytes 4718600 | tf_op jit(solution)/vmap(transpose(jvp()))/dot_general | solution.py:21
  1298.1 24.2 collective-permute-done.9
  1325.2 30.7 %collective-permute-start.10 = (f32[4096,96]{0,1:T(8,128)}, f32[4096,96]{0,1:T(8,128)S(1)}, u32[]{:S(2)}, u32[]{:S(2)}) collective-permute-start(f32[4096,96]{0,1:T(8,128)} %get-tuple-element.473), channel_id=18, source_target_pairs={{0,1},{1,2},{2,3},{3,4},{4,5},{5,6},{6,7},{7,8},{8,9},{9,10},{10,1... | collective-permute-start | bytes 4718600 | tf_op jit(solution)/vmap(transpose(jvp()))/dot_general | solution.py:21
  1536.8 17.7 collective-permute-start.26
  1554.5 51.5 %convert_multiply_fusion = (bf16[1,2048,4096]{2,1,0:T(8,128)(2,1)}, bf16[1,2048,4096]{2,1,0:T(8,128)(2,1)}) fusion(f32[2048,4096]{1,0:T(8,128)} %fusion.173, f32[2048,4096]{1,0:T(8,128)} %get-tuple-element.264, bf16[2,4096,1536]{2,1,0:T(8,128)(2,1)} %param.15, bf16[1,2048,1536]{1,2,0:T(8,128)(2,1)} %fusion.205), kind=kOutput, calls=%fused_computation.168 | convolution fusion | flops 25904021504 | bytes 119537664 | tf_op jit(solution)/vmap(transpose(jvp()))/dot_general | solution.py:9
  1606.0 324.9 %while.15 = (bf16[1,2048,4096]{2,1,0:T(8,128)(2,1)}, bf16[1,2048,1536]{1,2,0:T(8,128)(2,1)}, f32[4096,96]{0,1:T(8,128)S(1)}, f32[4096,96]{0,1:T(8,128)}, u32[]{:...) while((bf16[1,2048,4096]{2,1,0:T(8,128)(2,1)}, ...), condition=%wide.windowed_dot_general_cond_rs.3.clone, body=%wide.windowed_dot_general_body_rs.3.clone.sunk | while | flops 6447955968 | bytes 102761032 | solution.py:21
  1633.9 32.4 %collective-permute-start.14 = (f32[4096,96]{0,1:T(8,128)}, f32[4096,96]{0,1:T(8,128)}, u32[]{:S(2)}, u32[]{:S(2)}) collective-permute-start(f32[4096,96]{0,1:T(8,128)} %get-tuple-element.482), channel_id=24, source_target_pairs={{0,1},{1,2},{2,3},{3,4},{4,5},{5,6},{6,7},{7,8},{8,9},{9,10},{10,1... | collective-permute-start | bytes 4718600 | tf_op jit(solution)/vmap(transpose(jvp()))/dot_general | solution.py:21
  1851.9 17.5 collective-permute-start.12
  1959.6 396.3 %while.12 = (bf16[1,2048,4096]{2,1,0:T(8,128)(2,1)}, bf16[1,2048,1536]{1,2,0:T(8,128)(2,1)}, f32[4096,96]{0,1:T(8,128)S(1)}, f32[4096,96]{0,1:T(8,128)}, u32[]{:...) while((bf16[1,2048,4096]{2,1,0:T(8,128)(2,1)}, ...), condition=%wide.windowed_dot_general_cond_rs.clone, body=%wide.windowed_dot_general_body_rs.clone.sunk | while | flops 6447955968 | bytes 115344024 | solution.py:20
  1986.8 20.3 collective-permute-done.1
  2010.0 28.8 collective-permute-start.2
  2064.6 39.8 %collective-permute-start = (f32[4096,96]{0,1:T(8,128)}, f32[4096,96]{0,1:T(8,128)S(1)}, u32[]{:S(2)}, u32[]{:S(2)}) collective-permute-start(f32[4096,96]{0,1:T(8,128)} %broadcast_select_fusion.24), channel_id=3, source_target_pairs={{0,1},{1,2},{2,3},{3,4},{4,5},{5,6},{6,7},{7,8},{8,9},{9,10},{10,1... | collective-permute-start | bytes 4718600 | tf_op jit(solution)/vmap(transpose(jvp()))/dot_general | solution.py:20
  2114.6 19.8 collective-permute-done.1
  2137.3 31.2 %collective-permute-start.2 = (f32[4096,96]{0,1:T(8,128)}, f32[4096,96]{0,1:T(8,128)S(1)}, u32[]{:S(2)}, u32[]{:S(2)}) collective-permute-start(f32[4096,96]{0,1:T(8,128)} %get-tuple-element.455), channel_id=5, source_target_pairs={{0,1},{1,2},{2,3},{3,4},{4,5},{5,6},{6,7},{7,8},{8,9},{9,10},{10,1... | collective-permute-start | bytes 4718600 | tf_op jit(solution)/vmap(transpose(jvp()))/dot_general | solution.py:20
  2232.1 18.6 collective-permute-start.2
  2274.8 18.9 collective-permute-start
  2315.9 18.6 collective-permute-start.2
  2355.9 18.6 collective-permute-start.24
  2374.5 325.2 %while.13 = (bf16[1,2048,4096]{2,1,0:T(8,128)(2,1)}, bf16[1,2048,1536]{1,2,0:T(8,128)(2,1)}, f32[4096,96]{0,1:T(8,128)S(1)}, f32[4096,96]{0,1:T(8,128)}, u32[]{:...) while((bf16[1,2048,4096]{2,1,0:T(8,128)(2,1)}, ...), condition=%wide.windowed_dot_general_cond_rs.1.clone, body=%wide.windowed_dot_general_body_rs.1.clone.sunk | while | flops 6447955968 | bytes 102761032 | solution.py:20
  2402.0 32.4 %collective-permute-start.6 = (f32[4096,96]{0,1:T(8,128)}, f32[4096,96]{0,1:T(8,128)}, u32[]{:S(2)}, u32[]{:S(2)}) collective-permute-start(f32[4096,96]{0,1:T(8,128)} %get-tuple-element.464), channel_id=11, source_target_pairs={{0,1},{1,2},{2,3},{3,4},{4,5},{5,6},{6,7},{7,8},{8,9},{9,10},{10,1... | collective-permute-start | bytes 4718600 | tf_op jit(solution)/vmap(transpose(jvp()))/dot_general | solution.py:20
  2620.2 17.9 collective-permute-start.4
  2727.1 120.2 %all-gather.10.cloned.1.call-done = bf16[1,2,1536,4096]{3,2,1,0:T(8,128)(2,1)} async-done(((bf16[1,2,96,4096]{3,2,1,0:T(8,128)(2,1)}), bf16[1,2,1536,4096]{3,2,1,0:T(8,128)(2,1)}) %all-gather.10.cloned.1.call-update) | async-done | bytes 25165840 | tf_op jit(solution)/reshape | solution.py:52
  2847.2 23.0 copy.63
  2870.2 23.0 copy.64
  (442 shorter events, 1640.1 us)
Async XLA Ops:
  7.2 2719.8 %all-gather.14.cloned.1.call-start = ((), (), s32[]{:S(2)}) async-start(), calls=%async_computation.2 | async-start | bytes 26738688 | tf_op jit(solution)/reshape | solution.py:52
  356.4 38.5 %collective-permute-start.18 = (f32[256,1536]{1,0:T(8,128)}, f32[256,1536]{1,0:T(8,128)S(1)}, u32[]{:S(2)}, u32[]{:S(2)}) collective-permute-start(f32[256,1536]{1,0:T(8,128)} %get-tuple-element.491), channel_id=31, source_target_pairs={{0,1},{1,2},{2,3},{3,4},{4,5},{5,6},{6,7},{7,8},{8,9},{9,10},{10,1... | collective-permute-start | bytes 4718600 | tf_op jit(solution)/vmap(transpose(jvp()))/dot_general | solution.py:9
  412.5 23.6 collective-permute-start.16
  492.3 25.0 collective-permute-start.16
  573.5 25.2 collective-permute-start.16
  652.2 483.5 %collective-permute-start.28 = (f32[256,1536]{1,0:T(8,128)}, f32[256,1536]{1,0:T(8,128)}, u32[]{:S(2)}, u32[]{:S(2)}) collective-permute-start(f32[256,1536]{1,0:T(8,128)} %get-tuple-element.45), channel_id=32, source_target_pairs={{0,1},{1,2},{2,3},{3,4},{4,5},{5,6},{6,7},{7,8},{8,9},{9,10},{10,1... | collective-permute-start | bytes 4718600 | tf_op jit(solution)/vmap(transpose(jvp()))/dot_general | solution.py:9
  820.0 38.5 %collective-permute-start.22 = (f32[1536,256]{0,1:T(8,128)}, f32[1536,256]{0,1:T(8,128)}, u32[]{:S(2)}, u32[]{:S(2)}) collective-permute-start(f32[1536,256]{0,1:T(8,128)} %get-tuple-element.500), channel_id=37, source_target_pairs={{0,1},{1,2},{2,3},{3,4},{4,5},{5,6},{6,7},{7,8},{8,9},{9,10},{10,1... | collective-permute-start | bytes 4718600 | tf_op jit(solution)/vmap(transpose(jvp()))/dot_general | solution.py:9
  876.6 23.6 collective-permute-start.20
  956.5 24.8 collective-permute-start.20
  1038.4 25.3 collective-permute-start.20
  1147.0 1580.1 %all-gather.12.cloned.1.call-start = ((), (), s32[]{:S(2)}) async-start(), calls=%async_computation.1 | async-start | bytes 26738688 | tf_op jit(solution)/reshape | solution.py:52
  1148.5 24.6 collective-permute-start.8
  1165.3 29.2 %collective-permute-start.9 = (f32[4096,96]{0,1:T(8,128)}, f32[4096,96]{0,1:T(8,128)}, u32[]{:S(2)}, u32[]{:S(2)}) collective-permute-start(f32[4096,96]{0,1:T(8,128)} %broadcast_select_fusion.29), channel_id=15, source_target_pairs={{0,15},{1,0},{2,1},{3,2},{4,3},{5,4},{6,5},{7,6},{8,7},{9,8},{10,9... | collective-permute-start | bytes 4718600 | tf_op jit(solution)/vmap(transpose(jvp()))/dot_general | solution.py:21
  1197.5 39.5 %collective-permute-start.10 = (f32[4096,96]{0,1:T(8,128)}, f32[4096,96]{0,1:T(8,128)S(1)}, u32[]{:S(2)}, u32[]{:S(2)}) collective-permute-start(f32[4096,96]{0,1:T(8,128)} %get-tuple-element.473), channel_id=18, source_target_pairs={{0,1},{1,2},{2,3},{3,4},{4,5},{5,6},{6,7},{7,8},{8,9},{9,10},{10,1... | collective-permute-start | bytes 4718600 | tf_op jit(solution)/vmap(transpose(jvp()))/dot_general | solution.py:21
  1251.5 46.5 %collective-permute-start.8 = (f32[4096,96]{0,1:T(8,128)}, f32[4096,96]{0,1:T(8,128)S(1)}, u32[]{:S(2)}, u32[]{:S(2)}) collective-permute-start(f32[4096,96]{0,1:T(8,128)} %broadcast_select_fusion.28), channel_id=16, source_target_pairs={{0,1},{1,2},{2,3},{3,4},{4,5},{5,6},{6,7},{7,8},{8,9},{9,10},{10,1... | collective-permute-start | bytes 4718600 | tf_op jit(solution)/vmap(transpose(jvp()))/dot_general | solution.py:21
  1290.2 32.1 %collective-permute-start.9 = (f32[4096,96]{0,1:T(8,128)}, f32[4096,96]{0,1:T(8,128)}, u32[]{:S(2)}, u32[]{:S(2)}) collective-permute-start(f32[4096,96]{0,1:T(8,128)} %broadcast_select_fusion.29), channel_id=15, source_target_pairs={{0,15},{1,0},{2,1},{3,2},{4,3},{5,4},{6,5},{7,6},{8,7},{9,8},{10,9... | collective-permute-start | bytes 4718600 | tf_op jit(solution)/vmap(transpose(jvp()))/dot_general | solution.py:21
  1325.2 38.5 %collective-permute-start.10 = (f32[4096,96]{0,1:T(8,128)}, f32[4096,96]{0,1:T(8,128)S(1)}, u32[]{:S(2)}, u32[]{:S(2)}) collective-permute-start(f32[4096,96]{0,1:T(8,128)} %get-tuple-element.473), channel_id=18, source_target_pairs={{0,1},{1,2},{2,3},{3,4},{4,5},{5,6},{6,7},{7,8},{8,9},{9,10},{10,1... | collective-permute-start | bytes 4718600 | tf_op jit(solution)/vmap(transpose(jvp()))/dot_general | solution.py:21
  1379.6 25.3 collective-permute-start.8
  1418.0 25.1 collective-permute-start.10
  1458.8 26.5 collective-permute-start.8
  1498.5 25.3 collective-permute-start.10
  1536.8 411.5 %collective-permute-start.26 = (f32[4096,96]{0,1:T(8,128)}, f32[4096,96]{0,1:T(8,128)}, u32[]{:S(2)}, u32[]{:S(2)}) collective-permute-start(f32[4096,96]{0,1:T(8,128)} %get-tuple-element.41), channel_id=19, source_target_pairs={{0,1},{1,2},{2,3},{3,4},{4,5},{5,6},{6,7},{7,8},{8,9},{9,10},{10,1... | collective-permute-start | bytes 4718600 | tf_op jit(solution)/vmap(transpose(jvp()))/dot_general | solution.py:21
  1633.9 40.2 %collective-permute-start.14 = (f32[4096,96]{0,1:T(8,128)}, f32[4096,96]{0,1:T(8,128)}, u32[]{:S(2)}, u32[]{:S(2)}) collective-permute-start(f32[4096,96]{0,1:T(8,128)} %get-tuple-element.482), channel_id=24, source_target_pairs={{0,1},{1,2},{2,3},{3,4},{4,5},{5,6},{6,7},{7,8},{8,9},{9,10},{10,1... | collective-permute-start | bytes 4718600 | tf_op jit(solution)/vmap(transpose(jvp()))/dot_general | solution.py:21
  1690.4 25.3 collective-permute-start.12
  1729.2 24.7 collective-permute-start.14
  1770.2 26.5 collective-permute-start.12
  1810.3 25.3 collective-permute-start.14
  1851.9 26.6 collective-permute-start.12
  1892.0 25.3 collective-permute-start.14
  1959.6 887.6 %all-gather.10.cloned.1.call-start = ((), (), s32[]{:S(2)}) async-start(), calls=%async_computation | async-start | bytes 26738688 | tf_op jit(solution)/reshape | solution.py:52
  1961.1 24.6 collective-permute-start
  1977.8 29.2 %collective-permute-start.1 = (f32[4096,96]{0,1:T(8,128)}, f32[4096,96]{0,1:T(8,128)S(1)}, u32[]{:S(2)}, u32[]{:S(2)}) collective-permute-start(f32[4096,96]{0,1:T(8,128)} %broadcast_select_fusion.25), channel_id=2, source_target_pairs={{0,15},{1,0},{2,1},{3,2},{4,3},{5,4},{6,5},{7,6},{8,7},{9,8},{10,9... | collective-permute-start | bytes 4718600 | tf_op jit(solution)/vmap(transpose(jvp()))/dot_general | solution.py:20
  2010.0 39.5 %collective-permute-start.2 = (f32[4096,96]{0,1:T(8,128)}, f32[4096,96]{0,1:T(8,128)S(1)}, u32[]{:S(2)}, u32[]{:S(2)}) collective-permute-start(f32[4096,96]{0,1:T(8,128)} %get-tuple-element.455), channel_id=5, source_target_pairs={{0,1},{1,2},{2,3},{3,4},{4,5},{5,6},{6,7},{7,8},{8,9},{9,10},{10,1... | collective-permute-start | bytes 4718600 | tf_op jit(solution)/vmap(transpose(jvp()))/dot_general | solution.py:20
  2064.6 48.9 %collective-permute-start = (f32[4096,96]{0,1:T(8,128)}, f32[4096,96]{0,1:T(8,128)S(1)}, u32[]{:S(2)}, u32[]{:S(2)}) collective-permute-start(f32[4096,96]{0,1:T(8,128)} %broadcast_select_fusion.24), channel_id=3, source_target_pairs={{0,1},{1,2},{2,3},{3,4},{4,5},{5,6},{6,7},{7,8},{8,9},{9,10},{10,1... | collective-permute-start | bytes 4718600 | tf_op jit(solution)/vmap(transpose(jvp()))/dot_general | solution.py:20
  2105.6 28.7 collective-permute-start.1
  2137.3 39.0 %collective-permute-start.2 = (f32[4096,96]{0,1:T(8,128)}, f32[4096,96]{0,1:T(8,128)S(1)}, u32[]{:S(2)}, u32[]{:S(2)}) collective-permute-start(f32[4096,96]{0,1:T(8,128)} %get-tuple-element.455), channel_id=5, source_target_pairs={{0,1},{1,2},{2,3},{3,4},{4,5},{5,6},{6,7},{7,8},{8,9},{9,10},{10,1... | collective-permute-start | bytes 4718600 | tf_op jit(solution)/vmap(transpose(jvp()))/dot_general | solution.py:20
  2192.6 26.5 collective-permute-start
  2232.1 26.4 collective-permute-start.2
  2274.8 28.0 collective-permute-start
  2315.9 26.4 collective-permute-start.2
  2355.9 361.3 %collective-permute-start.24 = (f32[4096,96]{0,1:T(8,128)}, f32[4096,96]{0,1:T(8,128)}, u32[]{:S(2)}, u32[]{:S(2)}) collective-permute-start(f32[4096,96]{0,1:T(8,128)} %get-tuple-element.37), channel_id=6, source_target_pairs={{0,1},{1,2},{2,3},{3,4},{4,5},{5,6},{6,7},{7,8},{8,9},{9,10},{10,1... | collective-permute-start | bytes 4718600 | tf_op jit(solution)/vmap(transpose(jvp()))/dot_general | solution.py:20
  2402.0 40.2 %collective-permute-start.6 = (f32[4096,96]{0,1:T(8,128)}, f32[4096,96]{0,1:T(8,128)}, u32[]{:S(2)}, u32[]{:S(2)}) collective-permute-start(f32[4096,96]{0,1:T(8,128)} %get-tuple-element.464), channel_id=11, source_target_pairs={{0,1},{1,2},{2,3},{3,4},{4,5},{5,6},{6,7},{7,8},{8,9},{9,10},{10,1... | collective-permute-start | bytes 4718600 | tf_op jit(solution)/vmap(transpose(jvp()))/dot_general | solution.py:20
  2458.5 25.3 collective-permute-start.4
  2497.4 24.9 collective-permute-start.6
  2538.6 26.5 collective-permute-start.4
  2578.7 25.3 collective-permute-start.6
  2620.2 27.0 collective-permute-start.4
  2660.9 25.3 collective-permute-start.6
  (96 other events, 2429.8 us)
Sparse Core Ops, SparseCore 0:
  1147.1 204.1 all-gather.13
  1959.7 198.0 all-gather.11
  2727.1 120.0 all-gather.9
where the time goes:
time: 2920 us; the launch traced here: 2910 us
  starting transfers between devices  1030 us (35%)
  matrix products  717 us (25%)
  waiting for transfers between devices  685 us (23%)
  other arithmetic  318 us (11%)
  local copies, waits for them, and re-layouts  139 us (5%)
    dot_general x34, starting transfers between devices, layer(): gate = jnp.dot(a, w['w_gate'], preferred_element_type=jnp.float32)  364 us
    dot_general x34, starting transfers between devices, layer(): up = jnp.dot(a, w['w_up'], preferred_element_type=jnp.float32)  354 us
    dot_general x34, starting transfers between devices, matmul(): jnp.dot(a, w, preferred_element_type=jnp.float32).astype(jnp.bfloat16)  315 us
    dot_general x19, matrix products, layer(): gate = jnp.dot(a, w['w_gate'], preferred_element_type=jnp.float32)  251 us
    dot_general x19, matrix products, layer(): up = jnp.dot(a, w['w_up'], preferred_element_type=jnp.float32)  238 us
    dot_general x19, matrix products, matmul(): jnp.dot(a, w, preferred_element_type=jnp.float32).astype(jnp.bfloat16)  228 us
    dot_general x34, waiting for transfers between devices, layer(): up = jnp.dot(a, w['w_up'], preferred_element_type=jnp.float32)  193 us
    dot_general x34, waiting for transfers between devices, matmul(): jnp.dot(a, w, preferred_element_type=jnp.float32).astype(jnp.bfloat16)  192 us
  transfers between devices with their start and end apart: 105, of which 58 were waited for; matrix products, arithmetic and copies ran while one was open for 26% of the time, Pallas kernels for 0%

commit v1 on v0

v1 whole, which is shorter than its diff:
```python
import functools

import jax
import jax.numpy as jnp
from jax import lax
from jax.experimental import pallas as pl
from jax.experimental.pallas import tpu as pltpu
from jax.sharding import PartitionSpec as P

BF16, F32 = jnp.bfloat16, jnp.float32
BOTH = ("rep", "dp")
MESH = pl.DeviceIdType.MESH


def dot(a, b, ca, cb):
    return lax.dot_general(a, b, (((ca,), (cb,)), ((), ())), preferred_element_type=F32)


def scale_of(h):
    return lax.rsqrt(jnp.mean(h.astype(F32) ** 2, -1, keepdims=True) + 1e-6)


def hidden(gate, up):
    return (jax.nn.silu(gate) * up).astype(BF16)


def back_hidden(gate, up, by_act):
    by_act = by_act.astype(F32)
    s = jax.nn.sigmoid(gate)
    by_gate = by_act * up * (s * (1 + gate * (1 - s)))
    return by_gate.astype(BF16), (by_act * (gate * s)).astype(BF16)


def back_normed(h, scale, by_a):
    wide, by_a = h.astype(F32), by_a.astype(F32)
    by_scale = jnp.sum(by_a * wide, -1, keepdims=True)
    return (by_a * scale - wide * (by_scale * scale**3 / h.shape[-1])).astype(BF16)


ORDERS = ((0, 1, 2), (1, 2, 0), (2, 0, 1))
DOWN, HIDDEN = 8, 16
UNITS = DOWN + HIDDEN
LAG = 2
ARRIVE = 2 * LAG


def backward(save, number, *refs):
    dy_in, at_in, act_in, g_in, u_in, wd_in, out = refs[:7]
    saved, refs = refs[7 : 7 + 2 * save], refs[7 + 2 * save :]
    (dy, at, act, gate, up, wd, by_gate, by_up, whole, r1, s2, k2, r2, s3, k3, r3, s4, k4, r4) = refs[:19]
    loads, act_sem, in_sem, out_sem, send_sem, recv_sem = refs[19:]
    rep, me = lax.axis_index("rep"), lax.axis_index("dp")
    bits = [(me // (8 >> d)) % 2 for d in range(4)]
    near = [(rep, me + (8 >> d) * (1 - 2 * bits[d])) for d in range(4)]
    core = bits[3]

    def load(src, dst, sem):
        return pltpu.make_async_copy(src, dst, sem)

    def act_load(q):
        return load(act_in.at[:, q], act.at[q % 2], act_sem.at[q % 2])

    def hidden_loads(m):
        cols, slot = pl.ds(pl.multiple_of(m * 256, 256), 256), m % 2
        return (
            load(g_in.at[:, cols], gate.at[slot], in_sem.at[0, slot]),
            load(u_in.at[:, cols], up.at[slot], in_sem.at[1, slot]),
            load(wd_in.at[number, cols], wd.at[slot], in_sem.at[2, slot]),
        )

    def saves(m):
        cols, slot = pl.ds(pl.multiple_of(m * 256, 256), 256), m % 2
        return [
            load(src.at[slot], dst.at[:, cols], out_sem.at[i, slot])
            for i, (src, dst) in enumerate(zip((by_gate, by_up), saved))
        ]

    dy_load = load(dy_in, dy, loads.at[0])
    at_load = load(at_in, at, loads.at[1])
    act_load(0).start()
    dy_load.start()
    act_load(1).start()
    at_load.start()
    for one in hidden_loads(0):
        one.start()

    barrier = pltpu.get_barrier_semaphore()
    for neighbour in near:
        pl.semaphore_signal(barrier, inc=1, device_id=neighbour, device_id_type=MESH)
    pl.semaphore_wait(barrier, 4)

    def copy(i, src, dst, k, dim):
        return pltpu.make_async_remote_copy(
            src_ref=src,
            dst_ref=dst,
            send_sem=send_sem.at[i, k % ARRIVE],
            recv_sem=recv_sem.at[i, k % ARRIVE],
            device_id=near[dim],
            device_id_type=MESH,
        )

    def copies(stage, k):
        if stage == 0:
            return [copy(0, whole.at[k % (LAG + 1), :, 1 - core], r1.at[k % ARRIVE], k, 3)]
        src, dst = ((s2, r2), (s3, r3), (s4, r4))[stage - 1]
        return [
            copy(3 * stage - 2 + p, src.at[k % LAG, p], dst.at[k % ARRIVE, p], k, ORDERS[p][stage - 1]) for p in range(3)
        ]

    def take(stage, k):
        old, now, new = k % ARRIVE, k % LAG, k % (LAG + 1)
        for p, dims in enumerate(ORDERS):
            rows = slice(128 * p, 128 * p + 128)
            own = [bits[d] for d in dims]
            if stage == 0:
                for i in (0, 1):
                    for j in (0, 1):
                        for mine in (False, True):
                            at_bits = dict(zip(dims, (own[0] if mine else 1 - own[0], i, j)))
                            chip = at_bits[0] * 4 + at_bits[1] * 2 + at_bits[2]
                            both = whole[new, chip, core, rows].astype(F32) + r1[old, chip, rows].astype(F32)
                            if mine:
                                k2[now, p, i, j] = both
                            else:
                                s2[now, p, i, j] = both.astype(BF16)
            elif stage == 1:
                for j in (0, 1):
                    i = own[1]
                    s3[now, p, j] = (k2[now, p, 1 - i, j] + r2[old, p, 1 - i, j].astype(F32)).astype(BF16)
                    k3[now, p, j] = k2[now, p, i, j] + r2[old, p, i, j].astype(F32)
            elif stage == 2:
                j = own[2]
                s4[now, p] = (k3[now, p, 1 - j] + r3[old, p, 1 - j].astype(F32)).astype(BF16)
                k4[now, p] = k3[now, p, j] + r3[old, p, j].astype(F32)
            else:
                out[k, rows] = (k4[now, p] + r4[old, p].astype(F32)).astype(BF16)

    def step(n, _):
        for stage in (3, 2, 1, 0):
            k = n - 1 - LAG * (stage + 1)

            @pl.when((k >= 0) & (k < UNITS))
            def _():
                for one in copies(stage, k):
                    one.wait()
                take(stage, k)
                if stage < 3:
                    for one in copies(stage + 1, k):
                        one.start()

        @pl.when((n >= 1) & (n <= UNITS))
        def _():
            for one in copies(0, n - 1):
                one.start()

        slot = n % (LAG + 1)

        @pl.when(n < DOWN)
        def _():
            q = n // 2

            @pl.when(n == 0)
            def _():
                dy_load.wait()

            @pl.when(n % 2 == 0)
            def _():
                act_load(q).wait()

            cols = pl.ds(pl.multiple_of((n % 2) * 768, 768), 768)

            def block(b, _):
                rows = act[q % 2, pl.ds(b * 8, 8)].reshape(512, 2048)
                g = jnp.dot(rows, dy[:, cols], preferred_element_type=F32).astype(BF16)
                for i in range(8):
                    for c in range(6):
                        whole[slot, b * 4 + i // 2, i % 2, 64 * c : 64 * c + 64] = g[
                            64 * i : 64 * i + 64, 128 * c : 128 * c + 128
                        ]

            lax.fori_loop(0, 2, block, None)

            @pl.when((n % 2 == 1) & (q < 2))
            def _():
                act_load(q + 2).start()

        @pl.when((n >= DOWN) & (n < UNITS))
        def _():
            m = n - DOWN
            here = m % 2

            @pl.when(m == 0)
            def _():
                at_load.wait()

            for one in hidden_loads(m):
                one.wait()

            @pl.when(m < HIDDEN - 1)
            def _():
                for one in hidden_loads(m + 1):
                    one.start()

            if save:

                @pl.when(m >= 2)
                def _():
                    for one in saves(m - 2):
                        one.wait()

            def tokens(b, _):
                rows = pl.ds(pl.multiple_of(b * 512, 512), 512)
                by_act = lax.dot_general(dy[rows], wd[here], (((1,), (1,)), ((), ())), preferred_element_type=F32)
                by_g, by_u = back_hidden(gate[here, rows], up[here, rows], by_act.astype(BF16))
                by_gate[here, rows] = by_g
                by_up[here, rows] = by_u

            lax.fori_loop(0, 4, tokens, None)

            def block(b, _):
                rows = at[pl.ds(pl.multiple_of(b * 384, 384), 384)]
                for t, src in enumerate((by_gate, by_up)):
                    g = jnp.dot(rows, src[here], preferred_element_type=F32).astype(BF16)
                    for i in range(4):
                        for c in range(2):
                            lo = 192 * t + 96 * c
                            whole[slot, b * 2 + i // 2, i % 2, lo : lo + 96] = g[
                                96 * i : 96 * i + 96, 128 * c : 128 * c + 128
                            ]

            lax.fori_loop(0, 4, block, None)
            if save:
                for one in saves(m):
                    one.start()

    lax.fori_loop(0, UNITS + 1 + 4 * LAG, step, None)
    if save:
        for m in (HIDDEN - 2, HIDDEN - 1):
            for one in saves(m):
                one.wait()


def gradients(number, dy, a, act, gate, up, w_down, save):
    tokens, d = dy.shape
    ff = act.shape[1]
    any_, vmem = pl.BlockSpec(memory_space=pl.ANY), pl.BlockSpec(memory_space=pltpu.VMEM)
    out_shape = [jax.ShapeDtypeStruct((UNITS, 384, 128), BF16)]
    if save:
        out_shape += [jax.ShapeDtypeStruct((tokens, ff), BF16)] * 2

    def block(dtype, *shape):
        return pltpu.VMEM((*shape, 128, 128), dtype)

    out = pl.pallas_call(
        functools.partial(backward, save, number),
        out_shape=out_shape,
        in_specs=[any_] * 6,
        out_specs=[vmem] + [any_] * (2 * save),
        scratch_shapes=[
            pltpu.VMEM((tokens, d), BF16),
            pltpu.VMEM((d, tokens), BF16),
            pltpu.VMEM((2, 16, 64, tokens), BF16),
            pltpu.VMEM((2, tokens, 256), F32),
            pltpu.VMEM((2, tokens, 256), F32),
            pltpu.VMEM((2, 256, d), BF16),
            pltpu.VMEM((2, tokens, 256), BF16),
            pltpu.VMEM((2, tokens, 256), BF16),
            pltpu.VMEM((LAG + 1, 8, 2, 384, 128), BF16),
            pltpu.VMEM((ARRIVE, 8, 384, 128), BF16),
            block(BF16, LAG, 3, 2, 2),
            block(F32, LAG, 3, 2, 2),
            block(BF16, ARRIVE, 3, 2, 2),
            block(BF16, LAG, 3, 2),
            block(F32, LAG, 3, 2),
            block(BF16, ARRIVE, 3, 2),
            block(BF16, LAG, 3),
            block(F32, LAG, 3),
            block(BF16, ARRIVE, 3),
            pltpu.SemaphoreType.DMA((2,)),
            pltpu.SemaphoreType.DMA((2,)),
            pltpu.SemaphoreType.DMA((3, 2)),
            pltpu.SemaphoreType.DMA((2, 2)),
            pltpu.SemaphoreType.DMA((10, ARRIVE)),
            pltpu.SemaphoreType.DMA((10, ARRIVE)),
        ],
        compiler_params=pltpu.CompilerParams(
            collective_id=number, has_side_effects=True, vmem_limit_bytes=66_000_000
        ),
        cost_estimate=pl.CostEstimate(flops=8 * tokens * d * ff, bytes_accessed=200_000_000, transcendentals=tokens * ff),
    )(dy, a.T, act.T.reshape(16, 4, 64, tokens), gate, up, w_down)
    sums = out[0]
    down = sums[:DOWN].reshape(4, 2, 6, 64, 128).transpose(0, 3, 1, 2, 4).reshape(256, d)
    rest = sums[DOWN:].reshape(HIDDEN, 2, 2, 96, 128).transpose(1, 3, 0, 2, 4).reshape(2, 96, ff)
    return (rest[0], rest[1], down), out[1:]


def adamw(w, m, v, g):
    w, g = w.astype(F32), g.astype(F32)
    m = 0.9 * m + 0.1 * g
    v = 0.95 * v + 0.05 * g * g
    step = m * lax.rsqrt(v + 1e-8) + 0.1 * w
    return (w - 0.02 * step).astype(BF16), m, v


def solution(mesh):
    def compute(x, dy, *arrays):
        (wg, wu, wd), m, v = (arrays[i : i + 3] for i in (0, 3, 6))
        x, dy = x[0], dy[0]
        me = lax.axis_index("dp")
        new = [[None, None] for _ in range(3)]


        def finish(number, sums):
            for which, g in enumerate(sums):
                w, (rows, cols) = (wg, wu, wd)[which], g.shape
                own = lax.dynamic_slice(w, (number, me * rows, 0), (1, rows, cols))[0]
                new[which][number] = adamw(own, m[which][number], v[which][number], g)

        def gather(number):
            for which in (2, 0, 1):
                w, *moments = new[which][number]
                w = lax.all_gather(w, "dp", axis=0, tiled=True)
                new[which][number] = (w, *moments)

        s0 = scale_of(x)
        a0 = (x.astype(F32) * s0).astype(BF16)
        g0, u0 = dot(a0, wg[0], 1, 0), dot(a0, wu[0], 1, 0)
        act0 = hidden(g0, u0)
        h = x + dot(act0, wd[0], 1, 0).astype(BF16)
        s1 = scale_of(h)
        a1 = (h.astype(F32) * s1).astype(BF16)
        g1, u1 = dot(a1, wg[1], 1, 0), dot(a1, wu[1], 1, 0)
        sums, (by_g1, by_u1) = gradients(1, dy, a1, hidden(g1, u1), g1, u1, wd, True)
        finish(1, sums)
        ws = [one[1][0] for one in new]
        ws, by_g1, by_u1 = lax.optimization_barrier((ws, by_g1, by_u1))
        for one, w in zip(new, ws):
            one[1] = (w, *one[1][1:])
        gather(1)
        by_a1 = dot(by_g1, wg[1], 1, 1).astype(BF16) + dot(by_u1, wu[1], 1, 1).astype(BF16)
        by_h = dy + back_normed(h, s1, by_a1)
        sums, _ = gradients(0, by_h, a0, act0, g0, u0, wd, False)
        finish(0, sums)
        gather(0)
        return tuple(jnp.stack([one[n][k] for n in range(2)]) for k in range(3) for one in new)

    whole, rows = P(None, None, None), P(None, "dp", None)
    seq = P(BOTH, None, None)
    return jax.shard_map(
        compute,
        mesh=mesh,
        in_specs=(seq, seq, whole, whole, whole) + (rows,) * 6,
        out_specs=(P("rep", None, None),) * 3 + (P("rep", "dp", None),) * 6,
        check_vma=False,
    )
```

time: 2920 us -> 1190 us (0.41)
  starting transfers between devices: 1030 us -> 0.24 us
  matrix products: 717 us -> 270 us
  waiting for transfers between devices: 685 us -> 289 us
  Pallas kernels: 0 us -> 352 us
  other arithmetic: 318 us -> 133 us
    dot_general x102 -> x0, starting transfers between devices: 1030 us -> none  [the longest x34 364 us: layer(): gate = jnp.dot(a, w['w_gate'], preferred_element_type=jnp.float32)]
    dot_general x102 -> x0, waiting for transfers between devices: 565 us -> none  [the longest x34 193 us: layer(): up = jnp.dot(a, w['w_up'], preferred_element_type=jnp.float32)]
    dot_general x57 -> x7, matrix products: 717 us -> 270 us  [dot(): lax.dot_general(a, b, (((ca,), (cb,)), ((), ())), preferred_element_type=...]
    pallas_call x0 -> x2, Pallas kernels: none -> 352 us  [gradients(): pl.pallas_call(functools.partial(backward, save, number), out_shape=out_s...]
    all_gather x0 -> x6, waiting for transfers between devices: none -> 287 us  [gather(): w = lax.all_gather(w, 'dp', axis=0, tiled=True)]
    dot_general x96 -> x0, other arithmetic: 244 us -> none
    reshape x3 -> x0, waiting for transfers between devices: 120 us -> none  [step(): t.reshape(-1, *t.shape[2:])]
    unnamed x70 -> x60, local copies, waits for them, and re-layouts: 130 us -> 23.2 us
  transfers between devices with their start and end apart: 105 -> 6, of which waited for: 58 -> 6; matrix products, arithmetic and copies ran while one was open for 26% -> 8% of each run, Pallas kernels for 0% -> 0%
where the time goes in v1:
time: 1190 us; the launch traced here: 1170 us
  Pallas kernels  352 us (30%)
  waiting for transfers between devices  289 us (24%)
  matrix products  270 us (23%)
  other arithmetic  133 us (11%)
  local copies, waits for them, and re-layouts  116 us (10%)
  between operations  14.9 us (1%)
    pallas_call x2, Pallas kernels, gradients(): pl.pallas_call(functools.partial(backward, save, number), out_shape=out_s...  352 us
    all_gather x6, waiting for transfers between devices, gather(): w = lax.all_gather(w, 'dp', axis=0, tiled=True)  287 us
    dot_general x7, matrix products, dot(): lax.dot_general(a, b, (((ca,), (cb,)), ((), ())), preferred_element_type=...  270 us
    another operation x9, other arithmetic, compute(): jnp.stack([one[n][k] for n in range(2)])  73 us
    convert_element_type x2, local copies, waits for them, and re-layouts, hidden(): return (jax.nn.silu(gate) * up).astype(BF16)  44.9 us
    convert_element_type x18, local copies, waits for them, and re-layouts, adamw(): w, g = (w.astype(F32), g.astype(F32))  32.9 us
  transfers between devices with their start and end apart: 6, of which 6 were waited for; matrix products, arithmetic and copies ran while one was open for 8% of the time, Pallas kernels for 0%

profile of v1, /device:TPU:0, one launch (start us, length us, event | category | flops | bytes accessed | tf_op | source)
XLA Modules:
  0.0 1174.5 jit_solution(10473681844970631835)
XLA Ops:
  7.2 8.7 copy.39
  15.9 4.3 fusion.9
  20.5 32.5 %fusion.27.refs_3_ = f32[2048,4096]{1,0:T(8,128)} fusion(bf16[2,1536,4096]{2,1,0:T(8,128)(2,1)} %param.13, bf16[1,2048,1536]{2,1,0:T(8,128)(2,1)S(1)} %copy-done.16, f32[2048]{0:T(1024)S(1)} %add_rsqrt_fusion.1), kind=kOutput, calls=%fused_computation.44 | convolution fusion | flops 25779240960 | bytes 52436992 | tf_op jit(solution)/shard_map/dot_general | solution.py:16
  53.0 41.9 %fusion = (bf16[4096,2048]{0,1:T(8,128)(2,1)}, f32[2048,4096]{1,0:T(8,128)}) fusion(f32[2048,4096]{1,0:T(8,128)} %fusion.27.refs_3_, bf16[2,1536,4096]{2,1,0:T(8,128)(2,1)} %param.14, bf16[1,2048,1536]{2,1,0:T(8,128)(2,1)} %param.11, f32[2048]{0:T(1024)S(1)} %add_rsqrt_fusion.1), kind=kOutput, calls=%fused_computation.1 | convolution fusion | flops 25829572608 | bytes 102768640 | tf_op jit(solution)/shard_map/dot_general | solution.py:16
  94.9 42.4 %fusion.13 = (f32[2048]{0:T(1024)S(1)}, bf16[2048,1536]{0,1:T(8,128)(2,1)}) fusion(bf16[2,4096,1536]{2,1,0:T(8,128)(2,1)} %refs_5_.3, f32[2048,4096]{1,0:T(8,128)} %get-tuple-element.54.refs_4_, f32[2048,4096]{1,0:T(8,128)} %fusion.27.refs_3_, bf16[1,2048,1536]{1,2,0:T(8,128)(2,1)} %copy.39), kind=kOutput, calls=%fused_computation.30 | convolution fusion | flops 25835862016 | bytes 92282880 | tf_op jit(solution)/shard_map/dot_general | solution.py:16
  137.3 34.1 %fusion.22.refs_3_ = f32[2048,4096]{1,0:T(8,128)} fusion(bf16[2,1536,4096]{2,1,0:T(8,128)(2,1)} %param.13, bf16[2048,1536]{0,1:T(8,128)(2,1)} %get-tuple-element.48, f32[2048]{0:T(1024)S(1)} %add_rsqrt_fusion), kind=kOutput, calls=%fused_computation.39 | convolution fusion | flops 25779240960 | bytes 52436992 | tf_op jit(solution)/shard_map/dot_general | solution.py:16
  171.5 4.4 fusion.55.refs_1_
  175.9 47.8 %fusion.4 = (bf16[4096,2048]{0,1:T(8,128)(2,1)}, f32[2048,4096]{1,0:T(8,128)}) fusion(f32[2048,4096]{1,0:T(8,128)} %fusion.22.refs_3_, bf16[2,1536,4096]{2,1,0:T(8,128)(2,1)} %param.14, bf16[2048,1536]{0,1:T(8,128)(2,1)} %get-tuple-element.48, f32[2048]{0:T(1024)S(1)} %add_rsqrt_fusion), kind=kOutput, calls=%fused_computation.8 | convolution fusion | flops 25829572608 | bytes 102768640 | tf_op jit(solution)/shard_map/dot_general | solution.py:16
  223.7 22.4 %copy.40 = bf16[4096,2048]{1,0:T(8,128)(2,1)} copy(bf16[4096,2048]{0,1:T(8,128)(2,1)} %get-tuple-element.49) | data formatting | bytes 33554432 | tf_op jit(solution)/shard_map/convert_element_type | solution.py:24
  246.1 177.6 %shard_map.178 = (bf16[24,384,128]{2,1,0:T(8,128)(2,1)}, bf16[2048,4096]{1,0:T(8,128)(2,1)}, bf16[2048,4096]{1,0:T(8,128)(2,1)}) custom-call(bf16[2048,1536]{1,0:T(8,128)(2,1)} %bitcast.180, bf16[1536,2048]{1,0:T(8,128)(2,1)} %fusion.55.refs_1_, bf16[16,4,64,2048]{3,2,1,0:T(8,128)(2,1)} %bitcast.172, f32[2048,4096]{1,0:T(8,128)} %fusion.22.refs_3_, ...), custom_call_target="tpu_custom_call" | custom-call | flops 103079215104 | bytes 200000000 | tf_op jit(solution)/shard_map/pallas_call | solution.py:254
  425.2 2.1 slice.95
  427.3 9.0 copy.38
  436.3 7.6 fusion.47.refs_1_
  445.4 2.4 reshape.300
  449.0 2.4 reshape.302
  453.8 4.4 fusion.66
  458.2 5.4 fusion.60
  463.6 34.0 %fusion.39 = bf16[2048,1536]{0,1:T(8,128)(2,1)} fusion(bf16[2048,4096]{1,0:T(8,128)(2,1)} %get-tuple-element.20, bf16[2,1536,4096]{2,1,0:T(8,128)(2,1)} %param.13), kind=kOutput, calls=%fused_computation.55 | convolution fusion | flops 25772949504 | bytes 35651584 | tf_op jit(solution)/shard_map/dot_general | solution.py:16
  497.6 36.9 %fusion.15 = (f32[2048]{0:T(1024)S(1)}, bf16[2048,1536]{0,1:T(8,128)(2,1)}) fusion(bf16[2048,1536]{0,1:T(8,128)(2,1)} %get-tuple-element.48, bf16[2048,1536]{0,1:T(8,128)(2,1)} %fusion.39, bf16[2048,4096]{1,0:T(8,128)(2,1)} %get-tuple-element.21, bf16[2,1536,4096]{2,1,0:T(8,128)(2,1)} %param.14), kind=kOutput, calls=%fused_computation.32 | convolution fusion | flops 25788676096 | bytes 48242688 | tf_op jit(solution)/shard_map/dot_general | solution.py:16
  534.5 11.7 fusion.46
  546.2 8.6 copy.46.refs_0_
  554.8 22.4 %copy.45 = bf16[4096,2048]{1,0:T(8,128)(2,1)} copy(bf16[4096,2048]{0,1:T(8,128)(2,1)} %get-tuple-element.53) | data formatting | bytes 33554432 | tf_op jit(solution)/shard_map/convert_element_type | solution.py:24
  577.2 174.6 %shard_map.179 = bf16[24,384,128]{2,1,0:T(8,128)(2,1)} custom-call(bf16[2048,1536]{1,0:T(8,128)(2,1)} %copy.46.refs_0_, bf16[1536,2048]{1,0:T(8,128)(2,1)} %fusion.47.refs_1_, bf16[16,4,64,2048]{3,2,1,0:T(8,128)(2,1)} %bitcast.173, f32[2048,4096]{1,0:T(8,128)} %fusion.27.refs_3_, f32[2048,4096]{1,0:T(8,128)} %get-tuple-element.54.refs_4_, ...), custom_call_target="tpu_custom_call" | custom-call | flops 103079215104 | bytes 200000000 | tf_op jit(solution)/shard_map/pallas_call | solution.py:254
  755.2 4.2 fusion.75
  763.1 2.4 reshape.307
  765.5 4.4 fusion.72
  773.1 3.8 fusion.69
  777.5 3.0 reshape.314
  782.0 3.4 reshape.312
  785.5 2.4 reshape.313
  787.9 2.4 reshape.310
  790.3 2.4 reshape.311
  792.7 6.1 multiply_add_fusion.1
  798.9 1.9 pad_maximum_fusion.8
  800.7 1.9 pad_maximum_fusion.5
  806.9 1.9 pad_maximum_fusion.7
  812.7 1.9 pad_maximum_fusion.6
  814.5 1.9 pad_maximum_fusion.4
  816.4 1.9 pad_maximum_fusion.3
  818.3 3.1 all-gather.15.cloned.1.call-done
  821.4 64.9 %all-gather.17.cloned.1.call-done = bf16[4096,1536]{1,0:T(8,128)(2,1)} async-done(((bf16[256,1536]{1,0:T(8,128)(2,1)}), bf16[4096,1536]{1,0:T(8,128)(2,1)}) %all-gather.17.cloned.1.call-update) | async-done | bytes 12582928 | tf_op jit(solution)/shard_map/all_gather | solution.py:322
  886.3 20.7 %pad_maximum_fusion.2 = bf16[2,4096,1536]{2,1,0:T(8,128)(2,1)} fusion(bf16[1,4096,1536]{2,1,0:T(8,128)(2,1)} %bitcast.175, bf16[1,4096,1536]{2,1,0:T(8,128)(2,1)} %bitcast.174), kind=kLoop, calls=%fused_computation.17 | loop fusion | flops 12582912 | bytes 50331648 | tf_op jit(solution)/shard_map/stack | solution.py:345
  907.0 44.8 %all-gather.11.cloned.1.call-done = bf16[1536,4096]{1,0:T(8,128)(2,1)} async-done(((bf16[96,4096]{1,0:T(8,128)(2,1)}), bf16[1536,4096]{1,0:T(8,128)(2,1)}) %all-gather.11.cloned.1.call-update) | async-done | bytes 12582928 | tf_op jit(solution)/shard_map/all_gather | solution.py:322
  951.8 64.8 %all-gather.13.cloned.1.call-done = bf16[1536,4096]{1,0:T(8,128)(2,1)} async-done(((bf16[96,4096]{1,0:T(8,128)(2,1)}), bf16[1536,4096]{1,0:T(8,128)(2,1)}) %all-gather.13.cloned.1.call-update) | async-done | bytes 12582928 | tf_op jit(solution)/shard_map/all_gather | solution.py:322
  1016.6 20.6 %pad_maximum_fusion.1 = bf16[2,1536,4096]{2,1,0:T(8,128)(2,1)} fusion(bf16[1,1536,4096]{2,1,0:T(8,128)(2,1)} %bitcast.177, bf16[1,1536,4096]{2,1,0:T(8,128)(2,1)} %bitcast.176), kind=kLoop, calls=%fused_computation.16 | loop fusion | flops 12582912 | bytes 50331648 | tf_op jit(solution)/shard_map/stack | solution.py:345
  1037.2 44.7 %all-gather.7.cloned.1.call-done = bf16[1536,4096]{1,0:T(8,128)(2,1)} async-done(((bf16[96,4096]{1,0:T(8,128)(2,1)}), bf16[1536,4096]{1,0:T(8,128)(2,1)}) %all-gather.7.cloned.1.call-update) | async-done | bytes 12582928 | tf_op jit(solution)/shard_map/all_gather | solution.py:322
  1081.9 64.8 %all-gather.9.cloned.1.call-done = bf16[1536,4096]{1,0:T(8,128)(2,1)} async-done(((bf16[96,4096]{1,0:T(8,128)(2,1)}), bf16[1536,4096]{1,0:T(8,128)(2,1)}) %all-gather.9.cloned.1.call-update) | async-done | bytes 12582928 | tf_op jit(solution)/shard_map/all_gather | solution.py:322
  1146.7 20.5 %pad_maximum_fusion = bf16[2,1536,4096]{2,1,0:T(8,128)(2,1)} fusion(bf16[1,1536,4096]{2,1,0:T(8,128)(2,1)} %bitcast.179, bf16[1,1536,4096]{2,1,0:T(8,128)(2,1)} %bitcast.178), kind=kLoop, calls=%fused_computation.15 | loop fusion | flops 12582912 | bytes 50331648 | tf_op jit(solution)/shard_map/stack | solution.py:345
  (92 shorter events, 27.3 us)
Async XLA Ops:
  7.2 814.2 %all-gather.15.cloned.1.call-start = ((), (), s32[]{:S(2)}) async-start(), calls=%async_computation.4 | async-start | bytes 13369344 | tf_op jit(solution)/shard_map/all_gather | solution.py:322
  15.9 4.6 copy-start.16
  20.5 32.5 %copy-start.27 = (f32[2048]{0:T(1024)}, f32[2048]{0:T(1024)S(1)}, u32[]{:S(2)}) copy-start(f32[2048]{0:T(1024)S(1)} %add_rsqrt_fusion.1) | copy-start | bytes 24580
  137.3 34.2 %copy-start.25 = (f32[2048]{0:T(1024)}, f32[2048]{0:T(1024)S(1)}, u32[]{:S(2)}) copy-start(f32[2048]{0:T(1024)S(1)} %get-tuple-element.47) | copy-start | bytes 24580
  137.3 38.6 %copy-start.23 = (f32[2048]{0:T(1024)}, f32[2048]{0:T(1024)S(1)}, u32[]{:S(2)}) copy-start(f32[2048]{0:T(1024)S(1)} %add_rsqrt_fusion) | copy-start | bytes 24580
  137.3 34.2 %copy-start = (bf16[2048,1536]{0,1:T(8,128)(2,1)S(1)}, bf16[2048,1536]{0,1:T(8,128)(2,1)}, u32[]{:S(2)}) copy-start(bf16[2048,1536]{0,1:T(8,128)(2,1)} %get-tuple-element.48) | copy-start | bytes 18874372
  427.3 9.0 copy-start.28
  445.4 2.4 copy-start.4
  449.0 2.4 copy-start.6
  449.0 2.4 copy-start.22
  451.9 1.8 copy-start.1
  453.8 4.4 copy-start.11
  497.6 36.9 %copy-start.26 = (f32[2048]{0:T(1024)S(1)}, f32[2048]{0:T(1024)}, u32[]{:S(2)}) copy-start(f32[2048]{0:T(1024)} %copy-done.25) | copy-start | bytes 24580
  497.6 36.9 %copy-start.24 = (f32[2048]{0:T(1024)S(1)}, f32[2048]{0:T(1024)}, u32[]{:S(2)}) copy-start(f32[2048]{0:T(1024)} %copy-done.23) | copy-start | bytes 24580
  751.8 1.1 slice-start
  753.4 1.8 copy-start.3
  759.5 126.8 %all-gather.17.cloned.1.call-start = ((), (), s32[]{:S(2)}) async-start(), calls=%async_computation.5 | async-start | bytes 13369344 | tf_op jit(solution)/shard_map/all_gather | solution.py:322
  760.2 1.4 slice-start.1
  760.2 191.6 %all-gather.11.cloned.1.call-start = ((), (), s32[]{:S(2)}) async-start(), calls=%async_computation.2 | async-start | bytes 13369344 | tf_op jit(solution)/shard_map/all_gather | solution.py:322
  763.1 2.4 copy-start.8
  770.0 246.6 %all-gather.13.cloned.1.call-start = ((), (), s32[]{:S(2)}) async-start(), calls=%async_computation.3 | async-start | bytes 13369344 | tf_op jit(solution)/shard_map/all_gather | solution.py:322
  770.5 311.4 %all-gather.7.cloned.1.call-start = ((), (), s32[]{:S(2)}) async-start(), calls=%async_computation | async-start | bytes 13369344 | tf_op jit(solution)/shard_map/all_gather | solution.py:322
  771.8 1.3 copy-start.9
  776.9 369.8 %all-gather.9.cloned.1.call-start = ((), (), s32[]{:S(2)}) async-start(), calls=%async_computation.1 | async-start | bytes 13369344 | tf_op jit(solution)/shard_map/all_gather | solution.py:322
  777.5 3.1 copy-start.2
  782.0 3.4 copy-start.7
  785.5 2.4 copy-start.10
  787.9 2.4 copy-start.5
  790.3 2.4 copy-start.17
  798.8 3.8 copy-start.20
  798.8 3.8 copy-start.21
  800.7 3.4 copy-start.12
  800.7 4.4 copy-start.13
  805.2 3.6 copy-start.18
  805.2 3.6 copy-start.19
  806.8 3.2 copy-start.14
  806.8 4.2 copy-start.15
Sparse Core Ops, SparseCore 0:
  759.6 61.7 all-gather.14
  823.6 62.6 all-gather.16
  889.1 62.6 all-gather.10
  953.9 62.6 all-gather.12
  1019.2 62.6 all-gather.6
  1084.0 62.6 all-gather.8

commit v2 on v1

--- a/solution.py
+++ b/solution.py
@@ -12,10 +12,6 @@
 MESH = pl.DeviceIdType.MESH
 
 
-def dot(a, b, ca, cb):
-    return lax.dot_general(a, b, (((ca,), (cb,)), ((), ())), preferred_element_type=F32)
-
-
 def scale_of(h):
     return lax.rsqrt(jnp.mean(h.astype(F32) ** 2, -1, keepdims=True) + 1e-6)
 
@@ -38,17 +34,29 @@
 
 
 ORDERS = ((0, 1, 2), (1, 2, 0), (2, 0, 1))
-DOWN, HIDDEN = 8, 16
-UNITS = DOWN + HIDDEN
+COUNTS = (8, 16)
 LAG = 2
 ARRIVE = 2 * LAG
 
 
-def backward(save, number, *refs):
-    dy_in, at_in, act_in, g_in, u_in, wd_in, out = refs[:7]
-    saved, refs = refs[7 : 7 + 2 * save], refs[7 + 2 * save :]
-    (dy, at, act, gate, up, wd, by_gate, by_up, whole, r1, s2, k2, r2, s3, k3, r3, s4, k4, r4) = refs[:19]
-    loads, act_sem, in_sem, out_sem, send_sem, recv_sem = refs[19:]
+def backward(save, number, with_down, with_hidden, *refs):
+    DOWN, HIDDEN = COUNTS[0] * with_down, COUNTS[1] * with_hidden
+    UNITS = DOWN + HIDDEN
+    refs = list(refs)
+
+    def pop(wanted, n):
+        return [refs.pop(0) for _ in range(n)] if wanted else [None] * n
+
+    (dy_in,) = pop(True, 1)
+    (act_in,) = pop(with_down, 1)
+    at_in, g_in, u_in, wd_in = pop(with_hidden, 4)
+    (out,) = pop(True, 1)
+    saved = pop(save, 2)
+    (dy,) = pop(True, 1)
+    (act,) = pop(with_down, 1)
+    at, gate, up, wd, by_gate, by_up = pop(with_hidden, 6)
+    whole, r1, s2, k2, r2, s3, k3, r3, s4, k4, r4 = pop(True, 11)
+    loads, act_sem, in_sem, out_sem, send_sem, recv_sem = pop(True, 6)
     rep, me = lax.axis_index("rep"), lax.axis_index("dp")
     bits = [(me // (8 >> d)) % 2 for d in range(4)]
     near = [(rep, me + (8 >> d) * (1 - 2 * bits[d])) for d in range(4)]
@@ -76,13 +84,16 @@
         ]
 
     dy_load = load(dy_in, dy, loads.at[0])
-    at_load = load(at_in, at, loads.at[1])
-    act_load(0).start()
+    if with_down:
+        act_load(0).start()
     dy_load.start()
-    act_load(1).start()
-    at_load.start()
-    for one in hidden_loads(0):
-        one.start()
+    if with_down:
+        act_load(1).start()
+    if with_hidden:
+        for one in hidden_loads(0):
+            one.start()
+        at_load = load(at_in, at, loads.at[1])
+        at_load.start()
 
     barrier = pltpu.get_barrier_semaphore()
     for neighbour in near:
@@ -155,34 +166,38 @@
 
         slot = n % (LAG + 1)
 
-        @pl.when(n < DOWN)
+        @pl.when(n == 0)
         def _():
-            q = n // 2
-
-            @pl.when(n == 0)
+            dy_load.wait()
+
+        if with_down:
+            @pl.when(n < DOWN)
             def _():
-                dy_load.wait()
-
-            @pl.when(n % 2 == 0)
-            def _():
-                act_load(q).wait()
-
-            cols = pl.ds(pl.multiple_of((n % 2) * 768, 768), 768)
-
-            def block(b, _):
-                rows = act[q % 2, pl.ds(b * 8, 8)].reshape(512, 2048)
-                g = jnp.dot(rows, dy[:, cols], preferred_element_type=F32).astype(BF16)
-                for i in range(8):
-                    for c in range(6):
-                        whole[slot, b * 4 + i // 2, i % 2, 64 * c : 64 * c + 64] = g[
-                            64 * i : 64 * i + 64, 128 * c : 128 * c + 128
-                        ]
-
-            lax.fori_loop(0, 2, block, None)
-
-            @pl.when((n % 2 == 1) & (q < 2))
-            def _():
-                act_load(q + 2).start()
+                q = n // 2
+
+                @pl.when(n % 2 == 0)
+                def _():
+                    act_load(q).wait()
+
+                cols = pl.ds(pl.multiple_of((n % 2) * 768, 768), 768)
+
+                def block(b, _):
+                    rows = act[q % 2, pl.ds(b * 8, 8)].reshape(512, 2048)
+                    g = jnp.dot(rows, dy[:, cols], preferred_element_type=F32).astype(BF16)
+                    for i in range(8):
+                        for c in range(6):
+                            whole[slot, b * 4 + i // 2, i % 2, 64 * c : 64 * c + 64] = g[
+                                64 * i : 64 * i + 64, 128 * c : 128 * c + 128
+                            ]
+
+                lax.fori_loop(0, 2, block, None)
+
+                @pl.when((n % 2 == 1) & (q < 2))
+                def _():
+                    act_load(q + 2).start()
+
+        if not with_hidden:
+            return
 
         @pl.when((n >= DOWN) & (n < UNITS))
         def _():
@@ -240,31 +255,39 @@
                 one.wait()
 
 
-def gradients(number, dy, a, act, gate, up, w_down, save):
+def gradients(number, dy, a, act_t, gate, up, w_down, *, save=False, with_down=True, with_hidden=True, collective):
     tokens, d = dy.shape
-    ff = act.shape[1]
+    ff = w_down.shape[1]
     any_, vmem = pl.BlockSpec(memory_space=pl.ANY), pl.BlockSpec(memory_space=pltpu.VMEM)
-    out_shape = [jax.ShapeDtypeStruct((UNITS, 384, 128), BF16)]
+    down, hidden_ = COUNTS[0] * with_down, COUNTS[1] * with_hidden
+    out_shape = [jax.ShapeDtypeStruct((down + hidden_, 384, 128), BF16)]
     if save:
         out_shape += [jax.ShapeDtypeStruct((tokens, ff), BF16)] * 2
 
     def block(dtype, *shape):
         return pltpu.VMEM((*shape, 128, 128), dtype)
 
-    out = pl.pallas_call(
-        functools.partial(backward, save, number),
-        out_shape=out_shape,
-        in_specs=[any_] * 6,
-        out_specs=[vmem] + [any_] * (2 * save),
-        scratch_shapes=[
-            pltpu.VMEM((tokens, d), BF16),
+    operands, scratch = [dy], [pltpu.VMEM((tokens, d), BF16)]
+    if with_down:
+        operands.append(act_t.reshape(16, 4, 64, tokens))
+        scratch.append(pltpu.VMEM((2, 16, 64, tokens), BF16))
+    if with_hidden:
+        operands += [a.T, gate, up, w_down]
+        scratch += [
             pltpu.VMEM((d, tokens), BF16),
-            pltpu.VMEM((2, 16, 64, tokens), BF16),
             pltpu.VMEM((2, tokens, 256), F32),
             pltpu.VMEM((2, tokens, 256), F32),
             pltpu.VMEM((2, 256, d), BF16),
             pltpu.VMEM((2, tokens, 256), BF16),
             pltpu.VMEM((2, tokens, 256), BF16),
+        ]
+    out = pl.pallas_call(
+        functools.partial(backward, save, number, with_down, with_hidden),
+        out_shape=out_shape,
+        in_specs=[any_] * len(operands),
+        out_specs=[vmem] + [any_] * (2 * save),
+        scratch_shapes=scratch
+        + [
             pltpu.VMEM((LAG + 1, 8, 2, 384, 128), BF16),
             pltpu.VMEM((ARRIVE, 8, 384, 128), BF16),
             block(BF16, LAG, 3, 2, 2),
@@ -284,14 +307,121 @@
             pltpu.SemaphoreType.DMA((10, ARRIVE)),
         ],
         compiler_params=pltpu.CompilerParams(
-            collective_id=number, has_side_effects=True, vmem_limit_bytes=66_000_000
+            collective_id=collective, has_side_effects=True, vmem_limit_bytes=66_000_000
         ),
-        cost_estimate=pl.CostEstimate(flops=8 * tokens * d * ff, bytes_accessed=200_000_000, transcendentals=tokens * ff),
-    )(dy, a.T, act.T.reshape(16, 4, 64, tokens), gate, up, w_down)
-    sums = out[0]
-    down = sums[:DOWN].reshape(4, 2, 6, 64, 128).transpose(0, 3, 1, 2, 4).reshape(256, d)
-    rest = sums[DOWN:].reshape(HIDDEN, 2, 2, 96, 128).transpose(1, 3, 0, 2, 4).reshape(2, 96, ff)
-    return (rest[0], rest[1], down), out[1:]
+        cost_estimate=pl.CostEstimate(
+            flops=(2 * with_down + 6 * with_hidden) * tokens * d * ff,
+            bytes_accessed=100_000_000,
+            transcendentals=tokens * ff,
+        ),
+    )(*operands)
+    sums, found = out[0], {}
+    if with_down:
+        found[2] = sums[:down].reshape(4, 2, 6, 64, 128).transpose(0, 3, 1, 2, 4).reshape(256, d)
+    if with_hidden:
+        rest = sums[down:].reshape(hidden_, 2, 2, 96, 128).transpose(1, 3, 0, 2, 4).reshape(2, 96, ff)
+        found[0], found[1] = rest[0], rest[1]
+    return found, out[1:]
+
+
+def forward_hidden(number, a, w_gate, w_up, natural):
+    tokens, d = a.shape
+    ff, width = w_gate.shape[2], 256
+
+    def kernel(a_ref, wg_ref, wu_ref, gate_ref, up_ref, act_t_ref, *act_ref):
+        def block(b, _):
+            rows = pl.ds(pl.multiple_of(b * 512, 512), 512)
+            gate = jnp.dot(a_ref[rows], wg_ref[0], preferred_element_type=F32)
+            up = jnp.dot(a_ref[rows], wu_ref[0], preferred_element_type=F32)
+            gate_ref[rows] = gate
+            up_ref[rows] = up
+            act = hidden(gate, up)
+            act_t_ref[:, rows] = act.T
+            if natural:
+                act_ref[0][rows] = act
+
+        lax.fori_loop(0, tokens // 512, block, None)
+
+    wide = pl.BlockSpec((tokens, width), lambda i: (0, i))
+    weight = pl.BlockSpec((1, d, width), lambda i: (number, 0, i))
+    outs = [((tokens, ff), F32), ((tokens, ff), F32), ((ff, tokens), BF16)] + [((tokens, ff), BF16)] * natural
+    return pl.pallas_call(
+        kernel,
+        grid=(ff // width,),
+        out_shape=[jax.ShapeDtypeStruct(*one) for one in outs],
+        in_specs=[pl.BlockSpec((tokens, d), lambda i: (0, 0)), weight, weight],
+        out_specs=[wide, wide, pl.BlockSpec((width, tokens), lambda i: (i, 0))] + [wide] * natural,
+        compiler_params=pltpu.CompilerParams(vmem_limit_bytes=60_000_000),
+        cost_estimate=pl.CostEstimate(
+            flops=4 * tokens * d * ff, bytes_accessed=130_000_000, transcendentals=tokens * ff
+        ),
+    )(a, w_gate, w_up)
+
+
+def forward_down(number, x, act, w_down):
+    tokens, d = x.shape
+    ff, height = act.shape[1], 512
+
+    def kernel(x_ref, act_ref, wd_ref, h_ref, s_ref, a_ref):
+        for c in range(0, d, 512):
+            cols = slice(c, c + 512)
+            out = jnp.dot(act_ref[...], wd_ref[0, :, cols], preferred_element_type=F32).astype(BF16)
+            h_ref[:, cols] = x_ref[:, cols] + out
+        wide = h_ref[...].astype(F32)
+        scale = lax.rsqrt(jnp.mean(wide**2, -1, keepdims=True) + 1e-6)
+        s_ref[...] = scale
+        a_ref[...] = (wide * scale).astype(BF16)
+
+    def rows(n):
+        return pl.BlockSpec((height, n), lambda i: (i, 0))
+
+    return pl.pallas_call(
+        kernel,
+        name="forward_down",
+        grid=(tokens // height,),
+        out_shape=[
+            jax.ShapeDtypeStruct((tokens, d), BF16),
+            jax.ShapeDtypeStruct((tokens, 1), F32),
+            jax.ShapeDtypeStruct((tokens, d), BF16),
+        ],
+        in_specs=[rows(d), rows(ff), pl.BlockSpec((1, ff, d), lambda i: (number, 0, 0), pipeline_mode=pl.Buffered(1))],
+        out_specs=[rows(d), rows(1), rows(d)],
+        compiler_params=pltpu.CompilerParams(vmem_limit_bytes=60_000_000),
+        cost_estimate=pl.CostEstimate(flops=2 * tokens * d * ff, bytes_accessed=50_000_000, transcendentals=tokens),
+    )(x, act, w_down)
+
+
+def back_layer(number, by_gate, by_up, w_gate, w_up, h, scale, dy):
+    tokens, d = h.shape
+    ff, height = by_gate.shape[1], 512
+
+    def kernel(g_ref, u_ref, wg_ref, wu_ref, h_ref, s_ref, dy_ref, out_ref, by_a):
+        def part(c, _):
+            cols = pl.ds(pl.multiple_of(c * 512, 512), 512)
+            terms = [
+                lax.dot_general(t[...], w[0, cols], (((1,), (1,)), ((), ())), preferred_element_type=F32).astype(BF16)
+                for t, w in ((g_ref, wg_ref), (u_ref, wu_ref))
+            ]
+            by_a[:, cols] = terms[0] + terms[1]
+
+        lax.fori_loop(0, d // 512, part, None)
+        out_ref[...] = dy_ref[...] + back_normed(h_ref[...], s_ref[...], by_a[...])
+
+    def rows(n):
+        return pl.BlockSpec((height, n), lambda i: (i, 0))
+
+    weight = pl.BlockSpec((1, d, ff), lambda i: (number, 0, 0), pipeline_mode=pl.Buffered(1))
+    return pl.pallas_call(
+        kernel,
+        name="back_layer",
+        grid=(tokens // height,),
+        out_shape=jax.ShapeDtypeStruct((tokens, d), BF16),
+        in_specs=[rows(ff), rows(ff), weight, weight, rows(d), rows(1), rows(d)],
+        out_specs=rows(d),
+        scratch_shapes=[pltpu.VMEM((height, d), BF16)],
+        compiler_params=pltpu.CompilerParams(vmem_limit_bytes=64_000_000),
+        cost_estimate=pl.CostEstimate(flops=4 * tokens * d * ff, bytes_accessed=80_000_000, transcendentals=tokens),
+    )(by_gate, by_up, w_gate, w_up, h, scale, dy)
 
 
 def adamw(w, m, v, g):
@@ -311,37 +441,38 @@
 
 
         def finish(number, sums):
-            for which, g in enumerate(sums):
+            for which, g in sums.items():
                 w, (rows, cols) = (wg, wu, wd)[which], g.shape
                 own = lax.dynamic_slice(w, (number, me * rows, 0), (1, rows, cols))[0]
                 new[which][number] = adamw(own, m[which][number], v[which][number], g)
 
-        def gather(number):
-            for which in (2, 0, 1):
+        def gather(number, *names):
+            for which in names:
                 w, *moments = new[which][number]
                 w = lax.all_gather(w, "dp", axis=0, tiled=True)
                 new[which][number] = (w, *moments)
 
-        s0 = scale_of(x)
-        a0 = (x.astype(F32) * s0).astype(BF16)
-        g0, u0 = dot(a0, wg[0], 1, 0), dot(a0, wu[0], 1, 0)
-        act0 = hidden(g0, u0)
-        h = x + dot(act0, wd[0], 1, 0).astype(BF16)
-        s1 = scale_of(h)
-        a1 = (h.astype(F32) * s1).astype(BF16)
-        g1, u1 = dot(a1, wg[1], 1, 0), dot(a1, wu[1], 1, 0)
-        sums, (by_g1, by_u1) = gradients(1, dy, a1, hidden(g1, u1), g1, u1, wd, True)
+        def first(number, names, others):
+            ws, others = lax.optimization_barrier(([new[which][number][0] for which in names], others))
+            for which, w in zip(names, ws):
+                new[which][number] = (w, *new[which][number][1:])
+            gather(number, *names)
+            return others
+
+        a0 = (x.astype(F32) * scale_of(x)).astype(BF16)
+        g0, u0, act0_t, act0 = forward_hidden(0, a0, wg, wu, True)
+        h, s1, a1 = forward_down(0, x, act0, wd)
+        g1, u1, act1_t = forward_hidden(1, a1, wg, wu, False)
+        sums, by_hidden = gradients(1, dy, a1, act1_t, g1, u1, wd, save=True, collective=1)
         finish(1, sums)
-        ws = [one[1][0] for one in new]
-        ws, by_g1, by_u1 = lax.optimization_barrier((ws, by_g1, by_u1))
-        for one, w in zip(new, ws):
-            one[1] = (w, *one[1][1:])
-        gather(1)
-        by_a1 = dot(by_g1, wg[1], 1, 1).astype(BF16) + dot(by_u1, wu[1], 1, 1).astype(BF16)
-        by_h = dy + back_normed(h, s1, by_a1)
-        sums, _ = gradients(0, by_h, a0, act0, g0, u0, wd, False)
+        by_hidden = first(1, (2, 0, 1), by_hidden)
+        by_h = back_layer(1, *by_hidden, wg, wu, h, s1, dy)
+        sums, _ = gradients(0, by_h, None, act0_t, None, None, wd, with_hidden=False, collective=2)
         finish(0, sums)
-        gather(0)
+        by_h = first(0, (2,), by_h)
+        sums, _ = gradients(0, by_h, a0, None, g0, u0, wd, with_down=False, collective=3)
+        finish(0, sums)
+        gather(0, 0, 1)
         return tuple(jnp.stack([one[n][k] for n in range(2)]) for k in range(3) for one in new)
 
     whole, rows = P(None, None, None), P(None, "dp", None)

time: 1190 us -> 985 us (0.83)
  Pallas kernels: 352 us -> 662 us
  matrix products: 270 us -> 0 us
  waiting for transfers between devices: 289 us -> 101 us
  local copies, waits for them, and re-layouts: 116 us -> 73.6 us
    pallas_call x2 -> x7, Pallas kernels: 352 us -> 662 us  [the longest x3 405 us: gradients(): pl.pallas_call(functools.partial(backward, save, number, with_down, with_...]
    dot_general x7 -> x0, matrix products: 270 us -> none  [dot(): lax.dot_general(a, b, (((ca,), (cb,)), ((), ())), preferred_element_type=...]
    all_gather x6, waiting for transfers between devices: 287 us -> 99.4 us  [gather(): w = lax.all_gather(w, 'dp', axis=0, tiled=True)]
    convert_element_type x2 -> x1, local copies, waits for them, and re-layouts: 44.9 us -> 8.66 us  [compute(): a0 = (x.astype(F32) * scale_of(x)).astype(BF16)]
  transfers between devices with their start and end apart: 6 -> 6, of which waited for: 6 -> 2; matrix products, arithmetic and copies ran while one was open for 8% -> 11% of each run, Pallas kernels for 0% -> 31%
where the time goes in v2:
time: 985 us; the launch traced here: 975 us
  Pallas kernels  662 us (67%)
  other arithmetic  124 us (13%)
  waiting for transfers between devices  101 us (10%)
  local copies, waits for them, and re-layouts  73.6 us (7%)
  between operations  14.6 us (1%)
    pallas_call x3, Pallas kernels, gradients(): pl.pallas_call(functools.partial(backward, save, number, with_down, with_...  405 us
    pallas_call x2, Pallas kernels, forward_hidden(): pl.pallas_call(kernel, grid=(ff // width,), out_shape=[jax.ShapeDtypeStru...  147 us
    all_gather x6, waiting for transfers between devices, gather(): w = lax.all_gather(w, 'dp', axis=0, tiled=True)  99.4 us
    pallas_call x1, Pallas kernels, back_layer(): pl.pallas_call(kernel, name='back_layer', grid=(tokens // height,), out_s...  73.8 us
    another operation x9, other arithmetic, compute(): jnp.stack([one[n][k] for n in range(2)])  73.1 us
    pallas_call x1, Pallas kernels, forward_down(): pl.pallas_call(kernel, name='forward_down', grid=(tokens // height,), out...  35.9 us
    convert_element_type x18, local copies, waits for them, and re-layouts, adamw(): w, g = (w.astype(F32), g.astype(F32))  35.8 us
    convert_element_type x5, other arithmetic, adamw(): return ((w - 0.02 * step).astype(BF16), m, v)  22.9 us
  transfers between devices with their start and end apart: 6, of which 2 were waited for; matrix products, arithmetic and copies ran while one was open for 11% of the time, Pallas kernels for 31%

profile of v2, /device:TPU:0, one launch (start us, length us, event | category | flops | bytes accessed | tf_op | source)
XLA Modules:
  0.0 974.9 jit_solution(2092109795130547315)
XLA Ops:
  7.2 8.6 copy.36
  15.8 4.3 fusion
  20.7 4.6 fusion.1
  25.3 8.7 copy.37.a_ref
  34.0 73.7 %shard_map.178 = (f32[2048,4096]{1,0:T(8,128)}, f32[2048,4096]{1,0:T(8,128)}, bf16[4096,2048]{1,0:T(8,128)(2,1)}, bf16[2048,4096]{1,0:T(8,128)(2,1)}) custom-call(bf16[2048,1536]{1,0:T(8,128)(2,1)} %copy.37.a_ref, bf16[2,1536,4096]{2,1,0:T(8,128)(2,1)} %wg_ref.5, bf16[2,1536,4096]{2,1,0:T(8,128)(2,1)} %wu_ref.5), custom_call_target="tpu_custom_call" | custom-call | flops 51539607552 | bytes 130000000 | tf_op jit(solution)/shard_map/pallas_call | solution.py:348
  107.6 35.9 %forward_down.1 = (bf16[2048,1536]{1,0:T(8,128)(2,1)}, f32[2048,1]{1,0:T(8,128)}, bf16[2048,1536]{1,0:T(8,128)(2,1)}) custom-call(bf16[2048,1536]{1,0:T(8,128)(2,1)} %bitcast.98, bf16[2048,4096]{1,0:T(8,128)(2,1)} %get-tuple-element.29.act_ref, bf16[2,4096,1536]{2,1,0:T(8,128)(2,1)} %refs_4_.1), custom_call_target="tpu_custom_call" | custom-call | flops 25769803776 | bytes 50000000 | tf_op jit(solution)/shard_map/forward_down/pallas_call | solution.py:378
  143.6 8.7 copy.39
  152.3 73.2 %shard_map.179 = (f32[2048,4096]{1,0:T(8,128)}, f32[2048,4096]{1,0:T(8,128)}, bf16[4096,2048]{1,0:T(8,128)(2,1)}) custom-call(bf16[2048,1536]{1,0:T(8,128)(2,1)} %get-tuple-element.30.a_ref, bf16[2,1536,4096]{2,1,0:T(8,128)(2,1)} %wg_ref.5, bf16[2,1536,4096]{2,1,0:T(8,128)(2,1)} %wu_ref.5), custom_call_target="tpu_custom_call" | custom-call | flops 51539607552 | bytes 130000000 | tf_op jit(solution)/shard_map/pallas_call | solution.py:348
  225.5 177.7 %shard_map.180 = (bf16[24,384,128]{2,1,0:T(8,128)(2,1)}, bf16[2048,4096]{1,0:T(8,128)(2,1)}, bf16[2048,4096]{1,0:T(8,128)(2,1)}) custom-call(bf16[2048,1536]{1,0:T(8,128)(2,1)} %bitcast.104, bf16[16,4,64,2048]{3,2,1,0:T(8,128)(2,1)} %bitcast.107, bf16[1536,2048]{1,0:T(8,128)(2,1)} %bitcast.99, f32[2048,4096]{1,0:T(8,128)} %get-tuple-element.32.refs_3_, ...), custom_call_target="tpu_custom_call" | custom-call | flops 103079215104 | bytes 100000000 | tf_op jit(solution)/shard_map/pallas_call | solution.py:284
  404.3 2.7 slice.64
  407.5 1.7 reshape.265
  409.4 1.8 slice_convert_fusion.2
  413.6 2.4 reshape.267
  416.0 2.4 reshape.269
  418.4 4.4 fusion.4
  422.8 5.4 fusion.7
  428.3 73.8 %back_layer.1.refs_0_ = bf16[2048,1536]{1,0:T(8,128)(2,1)} custom-call(bf16[2048,4096]{1,0:T(8,128)(2,1)} %get-tuple-element.37.g_ref, bf16[2048,4096]{1,0:T(8,128)(2,1)} %get-tuple-element.38.u_ref, bf16[2,1536,4096]{2,1,0:T(8,128)(2,1)} %wg_ref.5, bf16[2,1536,4096]{2,1,0:T(8,128)(2,1)} %wu_ref.5, bf16[2048,1536]{1,0:T(8,128)(2,1)} %get-tuple-element.39.h_ref, ...), custom_call_target="tpu_custom_call" | custom-call | flops 51539607552 | bytes 80000000 | tf_op jit(solution)/shard_map/back_layer/pallas_call | solution.py:414
  502.1 61.3 %shard_map.181 = bf16[8,384,128]{2,1,0:T(8,128)(2,1)} custom-call(bf16[2048,1536]{1,0:T(8,128)(2,1)} %back_layer.1.refs_0_, bf16[16,4,64,2048]{3,2,1,0:T(8,128)(2,1)} %bitcast.106), custom_call_target="tpu_custom_call" | custom-call | flops 25769803776 | bytes 100000000 | tf_op jit(solution)/shard_map/pallas_call | solution.py:284
  563.4 1.6 copy.53
  565.1 1.7 reshape.270
  566.9 4.2 fusion.13
  571.9 7.7 fusion.50.refs_1_
  579.7 166.5 %shard_map.182 = bf16[16,384,128]{2,1,0:T(8,128)(2,1)} custom-call(bf16[2048,1536]{1,0:T(8,128)(2,1)} %back_layer.1.refs_0_, bf16[1536,2048]{1,0:T(8,128)(2,1)} %fusion.50.refs_1_, f32[2048,4096]{1,0:T(8,128)} %get-tuple-element.43.refs_2_, f32[2048,4096]{1,0:T(8,128)} %get-tuple-element.44.refs_3_, bf16[2,4096,1536]{2,1,0:T(8,128)(2,1)} %refs_4_.1), custom_call_target="tpu_custom_call" | custom-call | flops 77309411328 | bytes 100000000 | tf_op jit(solution)/shard_map/pallas_call | solution.py:284
  746.2 1.6 slice_convert_fusion
  749.0 2.4 reshape.271
  751.4 4.2 fusion.16
  758.7 2.4 reshape.273
  761.1 4.7 fusion.19
  767.3 3.5 reshape.275
  770.8 3.5 reshape.277
  775.8 3.4 reshape.274
  779.2 2.4 reshape.276
  781.6 4.5 multiply_add_fusion.1
  786.1 1.9 pad_maximum_fusion.5
  788.0 1.9 pad_maximum_fusion.8
  789.8 1.6 copy-done.11
  791.4 1.8 copy-done.12
  793.2 1.6 multiply_add_fusion.3
  794.9 1.9 pad_maximum_fusion.4
  796.8 1.9 pad_maximum_fusion.7
  801.2 1.6 multiply_add_fusion.5
  802.9 1.9 pad_maximum_fusion.3
  804.7 1.9 pad_maximum_fusion.6
  806.6 20.8 %pad_maximum_fusion.2 = bf16[2,4096,1536]{2,1,0:T(8,128)(2,1)} fusion(bf16[1,4096,1536]{2,1,0:T(8,128)(2,1)} %bitcast.92, bf16[1,4096,1536]{2,1,0:T(8,128)(2,1)} %bitcast.94), kind=kLoop, calls=%fused_computation.2 | loop fusion | flops 12582912 | bytes 50331648 | tf_op jit(solution)/shard_map/stack | solution.py:476
  827.4 20.6 %pad_maximum_fusion = bf16[2,1536,4096]{2,1,0:T(8,128)(2,1)} fusion(bf16[1,1536,4096]{2,1,0:T(8,128)(2,1)} %bitcast.93, bf16[1,1536,4096]{2,1,0:T(8,128)(2,1)} %bitcast.96), kind=kLoop, calls=%fused_computation | loop fusion | flops 12582912 | bytes 50331648 | tf_op jit(solution)/shard_map/stack | solution.py:476
  848.0 34.6 %all-gather.13.cloned.1.call-done = bf16[1536,4096]{1,0:T(8,128)(2,1)} async-done(((bf16[96,4096]{1,0:T(8,128)(2,1)}), bf16[1536,4096]{1,0:T(8,128)(2,1)}) %all-gather.13.cloned.1.call-update) | async-done | bytes 12582928 | tf_op jit(solution)/shard_map/all_gather | solution.py:452
  882.6 64.8 %all-gather.11.cloned.1.call-done = bf16[1536,4096]{1,0:T(8,128)(2,1)} async-done(((bf16[96,4096]{1,0:T(8,128)(2,1)}), bf16[1536,4096]{1,0:T(8,128)(2,1)}) %all-gather.11.cloned.1.call-update) | async-done | bytes 12582928 | tf_op jit(solution)/shard_map/all_gather | solution.py:452
  947.3 20.5 %pad_maximum_fusion.1 = bf16[2,1536,4096]{2,1,0:T(8,128)(2,1)} fusion(bf16[1,1536,4096]{2,1,0:T(8,128)(2,1)} %bitcast.95, bf16[1,1536,4096]{2,1,0:T(8,128)(2,1)} %bitcast.97), kind=kLoop, calls=%fused_computation.1 | loop fusion | flops 12582912 | bytes 50331648 | tf_op jit(solution)/shard_map/stack | solution.py:476
  (67 shorter events, 15.6 us)
Async XLA Ops:
  7.2 799.4 %all-gather.17.cloned.1.call-start = ((), (), s32[]{:S(2)}) async-start(), calls=%async_computation.5 | async-start | bytes 13369344 | tf_op jit(solution)/shard_map/all_gather | solution.py:452
  15.8 4.9 copy-start
  20.1 0.6 copy-start.20
  407.5 1.8 copy-start.1
  412.4 3.6 copy-start.5
  413.6 4.8 copy-start.6
  418.4 4.4 copy-start.10
  428.2 378.4 %all-gather.15.cloned.1.call-start = ((), (), s32[]{:S(2)}) async-start(), calls=%async_computation.4 | async-start | bytes 13369344 | tf_op jit(solution)/shard_map/all_gather | solution.py:452
  565.0 1.8 copy-start.3
  571.1 0.8 copy-start.21
  571.1 256.3 %all-gather.9.cloned.1.call-start = ((), (), s32[]{:S(2)}) async-start(), calls=%async_computation.1 | async-start | bytes 13369344 | tf_op jit(solution)/shard_map/all_gather | solution.py:452
  571.9 255.5 %all-gather.7.cloned.1.call-start = ((), (), s32[]{:S(2)}) async-start(), calls=%async_computation | async-start | bytes 13369344 | tf_op jit(solution)/shard_map/all_gather | solution.py:452
  749.0 6.6 copy-start.7
  755.7 126.9 %all-gather.13.cloned.1.call-start = ((), (), s32[]{:S(2)}) async-start(), calls=%async_computation.3 | async-start | bytes 13369344 | tf_op jit(solution)/shard_map/all_gather | solution.py:452
  756.3 191.1 %all-gather.11.cloned.1.call-start = ((), (), s32[]{:S(2)}) async-start(), calls=%async_computation.2 | async-start | bytes 13369344 | tf_op jit(solution)/shard_map/all_gather | solution.py:452
  757.5 1.1 copy-start.8
  761.1 4.7 copy-start.2
  770.8 3.5 copy-start.4
  775.8 3.4 copy-start.9
  779.2 2.4 copy-start.15
  786.1 3.8 copy-start.18
  786.1 3.8 copy-start.19
  788.0 3.4 copy-start.11
  788.0 5.2 copy-start.12
  794.9 3.8 copy-start.16
  794.9 3.8 copy-start.17
  796.8 3.3 copy-start.13
  796.8 4.4 copy-start.14
Sparse Core Ops, SparseCore 0:
  428.4 62.4 all-gather.16
  571.3 81.1 all-gather.14
  654.7 95.1 all-gather.8
  755.8 61.9 all-gather.6
  819.9 62.6 all-gather.12
  884.7 62.6 all-gather.10
